TPU v7x, 32 devices: a whole 2x2x4 slice. The times are simulated.
32 devices in a mesh: dp: 32 (over z, y, x, core).
Axes of the slice: x: 2, y: 2, z: 4, core: 2. Of those that a mesh axis runs over, the one named last changes fastest.
Arguments:
- tokens: bfloat16 [32768, 1024], P('dp'), may hold values from -80 to 80
- seg_ids: int32 [32, 1024], P('dp'), may hold values from 0 to 3, as said below
- counts: int32 [32], replicated, may hold values from 1 to 4, as said below
- positives: int32 [128], P('dp'), may hold values from 0 to 127, as said below
- w_qkv: bfloat16 [1024, 1536], replicated, may hold values from -0.1875 to 0.1875
- w_out: bfloat16 [512, 1024], replicated, may hold values from -0.25 to 0.25
- ln_gain: float32 [1024], replicated, may hold values from 0.1 to 1.9
- w_proj: bfloat16 [1024, 2048], replicated, may hold values from -0.1875 to 0.1875
Outputs:
- loss: float32 [128], P('dp')
- grad_pooled: float32 [128, 1024], P('dp')
Inputs may be any that keep to these rules, and one draw needn't show every extreme that they name: `seg_ids`: within a rank, the ids never fall and every id from 0 to 3 occurs. Rank r's live segments are its slots 0 to counts[r] - 1; the other slots hold padding; some rank has all 4 live. `positives`: a live slot of another rank, as rank times 4 plus slot.
All inputs are finite; a program needn't handle non-finite values.
Results may differ from a plain program's by a relative error of at most 0.008.
Values may be sent and summed in bfloat16 or wider, within the bound.
A program may use at most 192 MiB of HBM per device.

v0:
```python
import functools

import jax
import jax.numpy as jnp
from jax import lax
from jax.experimental import pallas as pl
from jax.experimental.pallas import tpu as pltpu
from jax.sharding import PartitionSpec as P

HEADS = 8
LOGIT_SCALE = 20.0
MESH = pl.DeviceIdType.MESH
F32 = jnp.float32
BF16 = jnp.bfloat16
EXT = 128
ONES_ROWS = 16
GROUP = 1024
LOG2E = 1.4426950408889634


def dot(a, b, ca, cb):
    return lax.dot_general(a, b, (((ca,), (cb,)), ((), ())), preferred_element_type=F32)


def attend_kernel(
    block, slots,
    counts_ref, pos_ref, seg_ref, gain_ref, tok_hbm, wqkv_hbm, wout_hbm,
    msg_ref,
    tok, wqkv, wout, qkv, vt, hot, far, ctx_t, ctx_new, s_buf, sums, sem_tok, sem_w,
):
    rows, width = tok.shape
    inner = wout.shape[0]
    head_dim = inner // HEADS
    blocks = rows // block
    me = lax.axis_index("dp")

    tok_copies = [
        pltpu.make_async_copy(
            tok_hbm.at[pl.ds(i * block, block)], tok.at[pl.ds(i * block, block)], sem_tok.at[i]
        )
        for i in range(blocks)
    ]
    w_copy = pltpu.make_async_copy(wqkv_hbm, wqkv, sem_w.at[0])
    o_copy = pltpu.make_async_copy(wout_hbm, wout, sem_w.at[1])
    tok_copies[0].start()
    w_copy.start()
    for c in tok_copies[1:]:
        c.start()
    o_copy.start()

    seg = seg_ref[...]
    lane = lax.broadcasted_iota(jnp.int32, (rows, 128), 1)
    seg_col = jnp.transpose(jnp.broadcast_to(seg.astype(F32), (128, rows))).astype(jnp.int32)
    hot[...] = jnp.where(seg_col == lane, 1.0, 0.0).astype(BF16)
    far[...] = jnp.where((lane < slots) & (seg_col != lane), -1e30, 0.0).astype(BF16)

    tok_copies[0].wait()
    w_copy.wait()
    for i in range(blocks):
        if i:
            tok_copies[i].wait()
        r = slice(i * block, (i + 1) * block)
        part = jnp.dot(tok[r, :], wqkv[...], preferred_element_type=F32).astype(BF16)
        qkv[r, :inner] = (part[:, :inner].astype(F32) * head_dim ** (-0.5)).astype(BF16)
        qkv[r, inner:] = part[:, inner : 2 * inner]
        vt[:, r] = jnp.transpose(part[:, 2 * inner :])

    o_copy.wait()
    sums[...] = jnp.zeros_like(sums)
    ctx_t[...] = jnp.zeros_like(ctx_t)
    ones = jnp.ones((ONES_ROWS, block), BF16)
    pair_lane = lax.broadcasted_iota(jnp.int32, (block, 128), 1)
    last = blocks - 1
    group = min(GROUP, rows)

    def query(h, i):
        qr = pl.ds(pl.multiple_of(i * block, block), block)
        lo = (h * head_dim) // 128 * 128
        own = (pair_lane >= h * head_dim - lo) & (pair_lane < (h + 1) * head_dim - lo)
        q = jnp.where(own, qkv[qr, lo : lo + 128], jnp.zeros((), BF16))
        return jnp.concatenate([q, far[qr, :]], axis=1)

    def score(h, g, q_ext, buf):
        r = slice(g * group, (g + 1) * group)
        lo = inner + (h * head_dim) // 128 * 128
        k_ext = jnp.concatenate([qkv[r, lo : lo + 128], hot[r, :]], axis=1)
        part = dot(k_ext, q_ext, 1, 1)
        s_buf[buf, r, :] = part
        return jnp.max(part, axis=0, keepdims=True)

    def finish(i, keep, half):
        rows_half = block // 2
        qr = pl.ds(pl.multiple_of(i * block + half * rows_half, rows_half), rows_half)
        ctx = ctx_t[:, half * rows_half : (half + 1) * rows_half]
        resid = tok[qr, :].astype(F32) + dot(ctx, wout[...], 0, 0)
        centre = resid - jnp.mean(resid, axis=-1, keepdims=True)
        variance = jnp.mean(centre * centre, axis=-1, keepdims=True)
        hidden = (centre * lax.rsqrt(variance + 1e-05) * gain_ref[...]).astype(BF16)
        slot = lax.broadcasted_iota(jnp.int32, (8, rows_half), 0)
        member = jnp.where((slot == seg_ref[:, qr]) & keep, 1.0, 0.0).astype(BF16)
        sums[...] += jnp.dot(member, hidden, preferred_element_type=F32)

    q_first = query(0, 0)
    top_first = functools.reduce(
        jnp.maximum, [score(0, g, q_first, 0) for g in range(rows // group)]
    )

    def step(i, top):
        prev = jnp.maximum(i - 1, 0)
        for h in range(HEADS):
            nxt = (h + 1) % HEADS
            q_ext = query(nxt, i if nxt else jnp.minimum(i + 1, last))
            hr = slice(h * head_dim, (h + 1) * head_dim)
            tops = []
            o = None
            for c in range(blocks):
                r = slice(c * block, (c + 1) * block)
                if c % (group // block) == 0:
                    tops.append(score(nxt, c * block // group, q_ext, nxt % 2))
                p = jnp.exp2((s_buf[h % 2, r, :] - top) * LOG2E).astype(BF16)
                v_ext = jnp.concatenate([vt[hr, r], ones], axis=0)
                part = jnp.dot(v_ext, p, preferred_element_type=F32)
                o = part if o is None else o + part
            top = functools.reduce(jnp.maximum, tops)
            ctx_new[hr, :] = (o[:head_dim] / o[head_dim : head_dim + 1]).astype(BF16)
            if h == 1:
                finish(prev, i > 0, 0)
            if h == 4:
                finish(prev, i > 0, 1)
        ctx_t[...] = ctx_new[...]
        return top

    lax.fori_loop(0, blocks, step, top_first)
    finish(last, True, 0)
    finish(last, True, 1)

    slot = lax.broadcasted_iota(jnp.int32, (8, rows), 0)
    sizes = jnp.sum(jnp.where(slot == seg, 1.0, 0.0), axis=1, keepdims=True)
    pooled = (sums[...] / jnp.maximum(sizes, 1.0)).astype(BF16)
    msg_ref[:, :width] = pooled[:slots]
    row = lax.broadcasted_iota(jnp.int32, (slots, EXT), 0)
    col = lax.broadcasted_iota(jnp.int32, (slots, EXT), 1)
    ext = jnp.where((col == 2) & (row < counts_ref[me]), 1, 0)
    for s in range(slots):
        p_rank = pos_ref[s] // slots
        p_slot = pos_ref[s] - p_rank * slots
        ext = jnp.where((row == s) & (col == 0), p_rank, ext)
        ext = jnp.where((row == s) & (col == 1), p_slot, ext)
    msg_ref[:, width:] = ext.astype(F32).astype(BF16)


def exchange_kernel(n, msg_ref, gath, send_sem, recv_sem, fwd_sem, got_sem, own_sem):
    me = lax.axis_index("dp")
    chips = n // 2
    core = lax.rem(me, 2)
    chip = me // 2
    other = chip * 2 + (1 - core)
    barrier = pltpu.get_barrier_semaphore()

    def peer_of(d):
        return lax.rem(chip + d, chips) * 2 + core

    def greet(d, c):
        pl.semaphore_signal(barrier, inc=1, device_id=(peer_of(d),), device_id_type=MESH)
        return c

    lax.fori_loop(1, chips, greet, 0)
    pl.semaphore_signal(barrier, inc=1, device_id=(other,), device_id_type=MESH)
    own = pltpu.make_async_copy(msg_ref, gath.at[me], own_sem)
    own.start()
    pl.semaphore_wait(barrier, chips)

    def send_to(d):
        return pltpu.make_async_remote_copy(
            src_ref=msg_ref, dst_ref=gath.at[me],
            send_sem=send_sem.at[d], recv_sem=recv_sem.at[d],
            device_id=(peer_of(d),), device_id_type=MESH,
        )

    def relay(d):
        src = lax.rem(chip + chips - d, chips) * 2 + core
        return pltpu.make_async_remote_copy(
            src_ref=gath.at[src], dst_ref=gath.at[src],
            send_sem=fwd_sem.at[d], recv_sem=got_sem.at[d],
            device_id=(other,), device_id_type=MESH,
        )

    mine = pltpu.make_async_remote_copy(
        src_ref=msg_ref, dst_ref=gath.at[me],
        send_sem=fwd_sem.at[0], recv_sem=got_sem.at[0],
        device_id=(other,), device_id_type=MESH,
    )

    def send(d, c):
        send_to(d).start()
        return c

    def forward(d, c):
        send_to(d).wait_recv()
        relay(d).start()
        return c

    def arrive(d, c):
        send_to(d).wait_send()
        relay(d).wait()
        return c

    lax.fori_loop(1, chips, send, 0)
    mine.start()
    lax.fori_loop(1, chips, forward, 0)
    own.wait()
    mine.wait()
    lax.fori_loop(1, chips, arrive, 0)


def loss_kernel(
    n, slots,
    gath, wproj,
    loss_ref, grad_ref,
    allp, unit, scale, wts, wts_t,
):
    me = lax.axis_index("dp")
    total = n * slots
    width = wproj.shape[0]
    per = 8 // slots

    def place(i, c):
        group = [gath[i * per + k].astype(F32) for k in range(per)]
        allp[pl.ds(pl.multiple_of(i * 8, 8), 8), :] = jnp.concatenate(group, axis=0)
        return c

    lax.fori_loop(0, total // 8, place, 0)

    pooled = allp[:, :width].astype(BF16)
    ext = allp[:, width:]
    proj = jnp.dot(pooled, wproj[...], preferred_element_type=F32)
    rnorm = lax.rsqrt(jnp.sum(proj * proj, axis=-1, keepdims=True) + 1e-06)
    unit_all = proj * rnorm
    unit[...] = unit_all
    scale[...] = jnp.broadcast_to(rnorm, scale.shape)
    emb = unit_all.astype(BF16)
    logits = LOGIT_SCALE * dot(emb, emb, 1, 1)

    row = lax.broadcasted_iota(jnp.int32, (total, total), 0)
    col = lax.broadcasted_iota(jnp.int32, (total, total), 1)
    pick = lax.broadcasted_iota(jnp.int32, (8, EXT), 1)
    live_row = dot(jnp.where(pick == 2, 1.0, 0.0).astype(BF16), ext.astype(BF16), 1, 1)[:1]
    live_col = ext[:, 2:3]
    positive = (ext[:, 0:1] * slots + ext[:, 1:2]).astype(jnp.int32)
    allowed = (live_row > 0.5) & (row != col)
    exp_logits = jnp.where(allowed, jnp.exp(logits), 0.0)
    denominator = jnp.sum(exp_logits, axis=-1, keepdims=True)
    target = col == positive
    picked = jnp.sum(jnp.where(target, logits, 0.0), axis=-1, keepdims=True)
    loss = jnp.where(live_col > 0.5, jnp.log(denominator) - picked, 0.0)
    mine = lax.broadcasted_iota(jnp.int32, (total, 128), 0) == (
        me * slots + lax.broadcasted_iota(jnp.int32, (total, 128), 1)
    )
    loss_ref[...] = jnp.sum(jnp.where(mine, loss, 0.0), axis=0)[:slots]
    weights = jnp.where(
        live_col > 0.5, exp_logits / denominator - jnp.where(target, 1.0, 0.0), 0.0
    )
    wts[...] = weights
    wts_t[...] = jnp.transpose(weights)

    base = pl.ds(pl.multiple_of(me // per * 8, 8), 8)
    d_emb = LOGIT_SCALE * (
        jnp.dot(wts[base, :].astype(BF16), emb, preferred_element_type=F32)
        + jnp.dot(wts_t[base, :].astype(BF16), emb, preferred_element_type=F32)
    )
    unit_own = unit[base, :]
    radial = jnp.sum(d_emb * unit_own, axis=-1, keepdims=True)
    d_proj = ((d_emb - radial * unit_own) * scale[base, :][:, :1]).astype(BF16)
    grad = dot(d_proj, wproj[...], 1, 1)
    part = lax.rem(me, per)
    out = grad[:slots]
    for k in range(1, per):
        out = jnp.where(part == k, grad[k * slots : (k + 1) * slots], out)
    grad_ref[...] = out


def body(n, tokens, seg_ids, counts, positives, w_qkv, w_out, ln_gain, w_proj):
    rows, width = tokens.shape
    slots = positives.shape[0]
    inner = w_out.shape[0]
    embed = w_proj.shape[1]
    block = min(256, rows)
    total = n * slots
    vmem = pl.BlockSpec(memory_space=pltpu.VMEM)
    smem = pl.BlockSpec(memory_space=pltpu.SMEM)
    hbm = pl.BlockSpec(memory_space=pl.ANY)
    msg = pl.pallas_call(
        functools.partial(attend_kernel, block, slots),
        name="attend",
        out_shape=jax.ShapeDtypeStruct((slots, width + EXT), BF16),
        in_specs=[smem, smem, vmem, vmem, hbm, hbm, hbm],
        out_specs=vmem,
        scratch_shapes=[
            pltpu.VMEM((rows, width), BF16),
            pltpu.VMEM(w_qkv.shape, BF16),
            pltpu.VMEM(w_out.shape, BF16),
            pltpu.VMEM((rows, 2 * inner), BF16),
            pltpu.VMEM((inner, rows), BF16),
            pltpu.VMEM((rows, 128), BF16),
            pltpu.VMEM((rows, 128), BF16),
            pltpu.VMEM((inner, block), BF16),
            pltpu.VMEM((inner, block), BF16),
            pltpu.VMEM((2, rows, block), F32),
            pltpu.VMEM((8, width), F32),
            pltpu.SemaphoreType.DMA((rows // block,)),
            pltpu.SemaphoreType.DMA((2,)),
        ],
        compiler_params=pltpu.CompilerParams(vmem_limit_bytes=56 * 1024 * 1024),
    )(counts, positives, seg_ids, ln_gain.reshape(1, width), tokens, w_qkv, w_out)
    gath = pl.pallas_call(
        functools.partial(exchange_kernel, n),
        name="exchange",
        out_shape=jax.ShapeDtypeStruct((n, slots, width + EXT), BF16),
        in_specs=[vmem],
        out_specs=vmem,
        scratch_shapes=[
            pltpu.SemaphoreType.DMA((n // 2,)),
            pltpu.SemaphoreType.DMA((n // 2,)),
            pltpu.SemaphoreType.DMA((n // 2,)),
            pltpu.SemaphoreType.DMA((n // 2,)),
            pltpu.SemaphoreType.DMA,
        ],
        compiler_params=pltpu.CompilerParams(
            collective_id=0, has_side_effects=True, vmem_limit_bytes=24 * 1024 * 1024
        ),
    )(msg)
    loss, grad = pl.pallas_call(
        functools.partial(loss_kernel, n, slots),
        name="contrast",
        out_shape=[
            jax.ShapeDtypeStruct((slots,), F32),
            jax.ShapeDtypeStruct((slots, width), F32),
        ],
        in_specs=[vmem, vmem],
        out_specs=[vmem, vmem],
        scratch_shapes=[
            pltpu.VMEM((total, width + EXT), F32),
            pltpu.VMEM((total, embed), F32),
            pltpu.VMEM((total, 128), F32),
            pltpu.VMEM((total, total), F32),
            pltpu.VMEM((total, total), F32),
        ],
        compiler_params=pltpu.CompilerParams(
            vmem_limit_bytes=(24 if total <= 128 else 56) * 1024 * 1024
        ),
    )(gath, w_proj)
    return loss, grad


def solution(mesh):
    return jax.shard_map(
        functools.partial(body, mesh.shape["dp"]),
        mesh=mesh,
        in_specs=(P("dp", None), P("dp", None), P(), P("dp"), P(), P(), P(), P()),
        out_specs=(P("dp"), P("dp", None)),
        check_vma=False,
    )
```

profile of v0, /device:TPU:0, one launch (start us, length us, event | category | flops | bytes accessed | tf_op | source)
XLA Modules:
  0.0 40.3 jit_solution(2754280290897246754)
XLA Ops:
  0.6 0.0 copy-start
  0.6 23.6 %attend.1.msg_ref = bf16[4,1152]{1,0:T(4,128)(2,1)} custom-call(s32[32]{0:T(128)} %counts_ref.1, s32[4]{0:T(128)} %pos_ref.1, s32[1,1024]{1,0:T(1,128)} %seg_ref.1, f32[1,1024]{1,0:T(1,128)} %bitcast.1, bf16[1024,1024]{1,0:T(8,128)(2,1)} %tok_hbm.1, bf16[1024,1536]{1,0:T(8,128)(2,1)} %wqkv_hbm.1, bf16[512,1024]{1,0:T(8,128)(2,1)} %wout_hbm.1), custom_call_target="tpu_custom_call" | custom-call | tf_op jit(solution)/shard_map/attend/pallas_call | solution.py:292
  24.2 0.0 copy-start.1
  24.2 0.7 %copy-done.1 = bf16[4,1152]{1,0:T(4,128)(2,1)S(1)} copy-done((bf16[4,1152]{1,0:T(4,128)(2,1)S(1)}, bf16[4,1152]{1,0:T(4,128)(2,1)}, u32[]{:S(2)}) %copy-start.1) | copy-done | bytes 9240
  24.9 11.6 %exchange.1.gath = bf16[32,4,1152]{2,1,0:T(4,128)(2,1)S(1)} custom-call(bf16[4,1152]{1,0:T(4,128)(2,1)S(1)} %copy-done.1), custom_call_target="tpu_custom_call" | custom-call | tf_op jit(solution)/shard_map/exchange/pallas_call | solution.py:315
  36.5 0.0 copy-done
  36.5 3.8 %contrast.1 = (f32[4]{0:T(128)}, f32[4,1024]{1,0:T(4,128)}) custom-call(bf16[32,4,1152]{2,1,0:T(4,128)(2,1)S(1)} %exchange.1.gath, bf16[1024,2048]{1,0:T(8,128)(2,1)S(1)} %copy-done), custom_call_target="tpu_custom_call" | custom-call | tf_op jit(solution)/shard_map/contrast/pallas_call | solution.py:332
Async XLA Ops:
  0.6 35.9 %copy-start = (bf16[1024,2048]{1,0:T(8,128)(2,1)S(1)}, bf16[1024,2048]{1,0:T(8,128)(2,1)}, u32[]{:S(2)}) copy-start(bf16[1024,2048]{1,0:T(8,128)(2,1)} %wproj.1) | copy-start | bytes 12582916
  24.2 0.7 %copy-start.1 = (bf16[4,1152]{1,0:T(4,128)(2,1)S(1)}, bf16[4,1152]{1,0:T(4,128)(2,1)}, u32[]{:S(2)}) copy-start(bf16[4,1152]{1,0:T(4,128)(2,1)} %attend.1.msg_ref) | copy-start | bytes 27652
where the time goes:
time: 40.5 us; the launch traced here: 40.3 us
  Pallas kernels  38.9 us (96%)
  local copies, waits for them, and re-layouts  0.7 us (2%)
  between operations  0.67 us (2%)
    pallas_call x1, Pallas kernels, body(): pl.pallas_call(functools.partial(attend_kernel, block, slots), name='atte...  23.6 us
    pallas_call x1, Pallas kernels, body(): pl.pallas_call(functools.partial(exchange_kernel, n), name='exchange', ou...  11.6 us
    pallas_call x1, Pallas kernels, body(): pl.pallas_call(functools.partial(loss_kernel, n, slots), name='contrast',...  3.76 us

commit v1 on v0

v1 whole, which is shorter than its diff:
```python
import functools

import jax
import jax.numpy as jnp
from jax import lax
from jax.experimental import pallas as pl
from jax.experimental.pallas import tpu as pltpu
from jax.sharding import PartitionSpec as P

HEADS = 8
LOGIT_SCALE = 20.0
MESH = pl.DeviceIdType.MESH
F32 = jnp.float32
BF16 = jnp.bfloat16
EXT = 128
ONES_ROWS = 16
GROUP = 1024
LOG2E = 1.4426950408889634


def dot(a, b, ca, cb):
    return lax.dot_general(a, b, (((ca,), (cb,)), ((), ())), preferred_element_type=F32)


def attend_kernel(
    block, slots,
    seg_hbm, tok_hbm, wqkv_hbm, wout_hbm,
    tok, wout, ctx_t,
    seg_ref, wqkv, qkv, vt, hot, far, s_buf, sem_tok, sem_w,
):
    rows, width = tok.shape
    inner = wout.shape[0]
    head_dim = inner // HEADS
    blocks = rows // block

    tok_copies = [
        pltpu.make_async_copy(
            tok_hbm.at[pl.ds(i * block, block)], tok.at[pl.ds(i * block, block)], sem_tok.at[i]
        )
        for i in range(blocks)
    ]
    w_copies = [
        pltpu.make_async_copy(
            wqkv_hbm.at[:, pl.ds(j * inner, inner)], wqkv.at[:, pl.ds(j * inner, inner)], sem_w.at[j]
        )
        for j in range(3)
    ]
    o_copy = pltpu.make_async_copy(wout_hbm, wout, sem_w.at[3])
    seg_copy = pltpu.make_async_copy(seg_hbm, seg_ref, sem_w.at[4])
    seg_copy.start()
    tok_copies[0].start()
    w_copies[0].start()
    for c in tok_copies[1:] + w_copies[1:]:
        c.start()
    o_copy.start()

    seg_copy.wait()
    seg = seg_ref[...]
    lane = lax.broadcasted_iota(jnp.int32, (rows, 128), 1)
    seg_col = jnp.transpose(jnp.broadcast_to(seg.astype(F32), (128, rows))).astype(jnp.int32)
    hot[...] = jnp.where(seg_col == lane, 1.0, 0.0).astype(BF16)
    far[...] = jnp.where((lane < slots) & (seg_col != lane), -1e30, 0.0).astype(BF16)
    starts = [
        jnp.sum(jnp.where(seg < s, 1.0, 0.0)).astype(jnp.int32) for s in range(1, slots)
    ]

    for j in range(3):
        w_copies[j].wait()
        cols = slice(j * inner, (j + 1) * inner)
        for i in range(blocks):
            if j == 0:
                tok_copies[i].wait()
            r = slice(i * block, (i + 1) * block)
            part = jnp.dot(tok[r, :], wqkv[:, cols], preferred_element_type=F32).astype(BF16)
            if j == 0:
                qkv[r, cols] = (part.astype(F32) * head_dim ** (-0.5)).astype(BF16)
            elif j == 1:
                qkv[r, cols] = part
            else:
                vt[:, r] = jnp.transpose(part)

    pair_lane = lax.broadcasted_iota(jnp.int32, (block, 128), 1)

    def attend(count, qr, base):
        bounds = [(c, min(c + block, count * 128)) for c in range(0, count * 128, block)]

        def query(h):
            lo = (h * head_dim) // 128 * 128
            own = (pair_lane >= h * head_dim - lo) & (pair_lane < (h + 1) * head_dim - lo)
            q = jnp.where(own, qkv[qr, lo : lo + 128], jnp.zeros((), BF16))
            return jnp.concatenate([q, far[qr, :]], axis=1)

        def score(h, q_ext, c):
            lo = inner + (h * head_dim) // 128 * 128
            a, b = bounds[c]
            kr = pl.ds(pl.multiple_of(base + a, 128), b - a)
            k_ext = jnp.concatenate([qkv[kr, lo : lo + 128], hot[kr, :]], axis=1)
            part = dot(k_ext, q_ext, 1, 1)
            s_buf[h % 2, a:b, :] = part
            return jnp.max(part, axis=0, keepdims=True)

        q_ext = query(0)
        top = functools.reduce(
            jnp.maximum, [score(0, q_ext, c) for c in range(len(bounds))]
        )
        for h in range(HEADS):
            hr = slice(h * head_dim, (h + 1) * head_dim)
            if h + 1 < HEADS:
                q_ext = query(h + 1)
            tops = []
            o = None
            for c, (a, b) in enumerate(bounds):
                if h + 1 < HEADS:
                    tops.append(score(h + 1, q_ext, c))
                p = jnp.exp2((s_buf[h % 2, a:b, :] - top) * LOG2E).astype(BF16)
                kr = pl.ds(pl.multiple_of(base + a, 128), b - a)
                v_ext = jnp.concatenate([vt[hr, kr], jnp.ones((ONES_ROWS, b - a), BF16)], axis=0)
                part = jnp.dot(v_ext, p, preferred_element_type=F32)
                o = part if o is None else o + part
            ctx_t[hr, qr] = (o[:head_dim] / o[head_dim : head_dim + 1]).astype(BF16)
            if tops:
                top = functools.reduce(jnp.maximum, tops)

    def step(i, carry):
        begin = i * block
        lo = jnp.int32(0)
        hi = jnp.int32(rows)
        for s in starts:
            lo = jnp.where(s <= begin, jnp.maximum(lo, s), lo)
            hi = jnp.where(s >= begin + block, jnp.minimum(hi, s), hi)
        first = lo // 128
        count = (hi + 127) // 128 - first
        qr = pl.ds(pl.multiple_of(begin, block), block)
        base = first * 128
        for n in range(block // 128, rows // 128 + 1):

            @pl.when(count == n)
            def _():
                attend(n, qr, base)

        return carry

    lax.fori_loop(0, blocks, step, 0)
    o_copy.wait()


def exchange_kernel(
    n, slots, block,
    counts_ref, pos_ref, seg_ref, gain_ref, tok, wout, ctx_t, wproj_hbm,
    gath, wproj,
    msg_ref, sums, send_sem, recv_sem, fwd_sem, got_sem, own_sem, w_sem,
):
    me = lax.axis_index("dp")
    chips = n // 2
    core = lax.rem(me, 2)
    chip = me // 2
    other = chip * 2 + (1 - core)
    rows, width = tok.shape
    barrier = pltpu.get_barrier_semaphore()

    def peer_of(d):
        return lax.rem(chip + d, chips) * 2 + core

    def greet(d, c):
        pl.semaphore_signal(barrier, inc=1, device_id=(peer_of(d),), device_id_type=MESH)
        return c

    lax.fori_loop(1, chips, greet, 0)
    pl.semaphore_signal(barrier, inc=1, device_id=(other,), device_id_type=MESH)
    w_copy = pltpu.make_async_copy(wproj_hbm, wproj, w_sem)
    w_copy.start()

    total_sum = None
    for i in range(rows // block):
        qr = slice(i * block, (i + 1) * block)
        resid = tok[qr, :].astype(F32) + dot(ctx_t[:, qr], wout[...], 0, 0)
        centre = resid - jnp.mean(resid, axis=-1, keepdims=True)
        variance = jnp.mean(centre * centre, axis=-1, keepdims=True)
        hidden = (centre * lax.rsqrt(variance + 1e-05) * gain_ref[...]).astype(BF16)
        slot = lax.broadcasted_iota(jnp.int32, (8, block), 0)
        member = jnp.where(slot == seg_ref[:, qr], 1.0, 0.0).astype(BF16)
        part = jnp.dot(member, hidden, preferred_element_type=F32)
        if i == 0:
            sums[...] = part
        else:
            sums[...] += part

    slot = lax.broadcasted_iota(jnp.int32, (8, rows), 0)
    sizes = jnp.sum(jnp.where(slot == seg_ref[...], 1.0, 0.0), axis=1, keepdims=True)
    pooled = (sums[...] / jnp.maximum(sizes, 1.0)).astype(BF16)
    msg_ref[:, :width] = pooled[:slots]
    row = lax.broadcasted_iota(jnp.int32, (slots, EXT), 0)
    col = lax.broadcasted_iota(jnp.int32, (slots, EXT), 1)
    ext = jnp.where((col == 2) & (row < counts_ref[me]), 1, 0)
    for s in range(slots):
        p_rank = pos_ref[s] // slots
        p_slot = pos_ref[s] - p_rank * slots
        ext = jnp.where((row == s) & (col == 0), p_rank, ext)
        ext = jnp.where((row == s) & (col == 1), p_slot, ext)
    msg_ref[:, width:] = ext.astype(F32).astype(BF16)

    pl.semaphore_wait(barrier, chips)
    own = pltpu.make_async_copy(msg_ref, gath.at[me], own_sem)
    own.start()

    def send_to(d):
        return pltpu.make_async_remote_copy(
            src_ref=msg_ref, dst_ref=gath.at[me],
            send_sem=send_sem.at[d], recv_sem=recv_sem.at[d],
            device_id=(peer_of(d),), device_id_type=MESH,
        )

    def relay(d):
        src = lax.rem(chip + chips - d, chips) * 2 + core
        return pltpu.make_async_remote_copy(
            src_ref=gath.at[src], dst_ref=gath.at[src],
            send_sem=fwd_sem.at[d], recv_sem=got_sem.at[d],
            device_id=(other,), device_id_type=MESH,
        )

    mine = pltpu.make_async_remote_copy(
        src_ref=msg_ref, dst_ref=gath.at[me],
        send_sem=fwd_sem.at[0], recv_sem=got_sem.at[0],
        device_id=(other,), device_id_type=MESH,
    )

    def send(d, c):
        send_to(d).start()
        return c

    def forward(d, c):
        send_to(d).wait_recv()
        relay(d).start()
        return c

    def arrive(d, c):
        send_to(d).wait_send()
        relay(d).wait()
        return c

    lax.fori_loop(1, chips, send, 0)
    mine.start()
    lax.fori_loop(1, chips, forward, 0)
    own.wait()
    mine.wait()
    lax.fori_loop(1, chips, arrive, 0)
    w_copy.wait()


def loss_kernel(
    n, slots,
    gath, wproj,
    loss_ref, grad_ref,
    allp, unit, scale, wts, wts_t,
):
    me = lax.axis_index("dp")
    total = n * slots
    width = wproj.shape[0]
    per = 8 // slots

    def place(i, c):
        group = [gath[i * per + k].astype(F32) for k in range(per)]
        allp[pl.ds(pl.multiple_of(i * 8, 8), 8), :] = jnp.concatenate(group, axis=0)
        return c

    lax.fori_loop(0, total // 8, place, 0)

    pooled = allp[:, :width].astype(BF16)
    ext = allp[:, width:]
    proj = jnp.dot(pooled, wproj[...], preferred_element_type=F32)
    rnorm = lax.rsqrt(jnp.sum(proj * proj, axis=-1, keepdims=True) + 1e-06)
    unit_all = proj * rnorm
    unit[...] = unit_all
    scale[...] = jnp.broadcast_to(rnorm, scale.shape)
    emb = unit_all.astype(BF16)
    logits = LOGIT_SCALE * dot(emb, emb, 1, 1)

    row = lax.broadcasted_iota(jnp.int32, (total, total), 0)
    col = lax.broadcasted_iota(jnp.int32, (total, total), 1)
    pick = lax.broadcasted_iota(jnp.int32, (8, EXT), 1)
    live_row = dot(jnp.where(pick == 2, 1.0, 0.0).astype(BF16), ext.astype(BF16), 1, 1)[:1]
    live_col = ext[:, 2:3]
    positive = (ext[:, 0:1] * slots + ext[:, 1:2]).astype(jnp.int32)
    allowed = (live_row > 0.5) & (row != col)
    exp_logits = jnp.where(allowed, jnp.exp(logits), 0.0)
    denominator = jnp.sum(exp_logits, axis=-1, keepdims=True)
    target = col == positive
    picked = jnp.sum(jnp.where(target, logits, 0.0), axis=-1, keepdims=True)
    loss = jnp.where(live_col > 0.5, jnp.log(denominator) - picked, 0.0)
    mine = lax.broadcasted_iota(jnp.int32, (total, 128), 0) == (
        me * slots + lax.broadcasted_iota(jnp.int32, (total, 128), 1)
    )
    loss_ref[...] = jnp.sum(jnp.where(mine, loss, 0.0), axis=0)[:slots]
    weights = jnp.where(
        live_col > 0.5, exp_logits / denominator - jnp.where(target, 1.0, 0.0), 0.0
    )
    wts[...] = weights
    wts_t[...] = jnp.transpose(weights)

    base = pl.ds(pl.multiple_of(me // per * 8, 8), 8)
    d_emb = LOGIT_SCALE * (
        jnp.dot(wts[base, :].astype(BF16), emb, preferred_element_type=F32)
        + jnp.dot(wts_t[base, :].astype(BF16), emb, preferred_element_type=F32)
    )
    unit_own = unit[base, :]
    radial = jnp.sum(d_emb * unit_own, axis=-1, keepdims=True)
    d_proj = ((d_emb - radial * unit_own) * scale[base, :][:, :1]).astype(BF16)
    grad = dot(d_proj, wproj[...], 1, 1)
    part = lax.rem(me, per)
    out = grad[:slots]
    for k in range(1, per):
        out = jnp.where(part == k, grad[k * slots : (k + 1) * slots], out)
    grad_ref[...] = out


def body(n, tokens, seg_ids, counts, positives, w_qkv, w_out, ln_gain, w_proj):
    rows, width = tokens.shape
    slots = positives.shape[0]
    inner = w_out.shape[0]
    embed = w_proj.shape[1]
    block = min(256, rows)
    total = n * slots
    vmem = pl.BlockSpec(memory_space=pltpu.VMEM)
    smem = pl.BlockSpec(memory_space=pltpu.SMEM)
    hbm = pl.BlockSpec(memory_space=pltpu.HBM)
    tokens, seg_hbm, w_qkv, w_out, w_proj = (
        pltpu.with_memory_space_constraint(a, pltpu.HBM)
        for a in (tokens, seg_ids, w_qkv, w_out, w_proj)
    )
    tok, wout, ctx_t = pl.pallas_call(
        functools.partial(attend_kernel, block, slots),
        name="attend",
        out_shape=[
            jax.ShapeDtypeStruct((rows, width), BF16),
            jax.ShapeDtypeStruct(w_out.shape, BF16),
            jax.ShapeDtypeStruct((inner, rows), BF16),
        ],
        in_specs=[hbm, hbm, hbm, hbm],
        out_specs=[vmem, vmem, vmem],
        scratch_shapes=[
            pltpu.VMEM((1, rows), jnp.int32),
            pltpu.VMEM(w_qkv.shape, BF16),
            pltpu.VMEM((rows, 2 * inner), BF16),
            pltpu.VMEM((inner, rows), BF16),
            pltpu.VMEM((rows, 128), BF16),
            pltpu.VMEM((rows, 128), BF16),
            pltpu.VMEM((2, rows, block), F32),
            pltpu.SemaphoreType.DMA((rows // block,)),
            pltpu.SemaphoreType.DMA((5,)),
        ],
        compiler_params=pltpu.CompilerParams(vmem_limit_bytes=32 * 1024 * 1024),
    )(seg_hbm, tokens, w_qkv, w_out)
    gath, wproj = pl.pallas_call(
        functools.partial(exchange_kernel, n, slots, block),
        name="exchange",
        out_shape=[
            jax.ShapeDtypeStruct((n, slots, width + EXT), BF16),
            jax.ShapeDtypeStruct(w_proj.shape, BF16),
        ],
        in_specs=[smem, smem, vmem, vmem, vmem, vmem, vmem, hbm],
        out_specs=[vmem, vmem],
        scratch_shapes=[
            pltpu.VMEM((slots, width + EXT), BF16),
            pltpu.VMEM((8, width), F32),
            pltpu.SemaphoreType.DMA((n // 2,)),
            pltpu.SemaphoreType.DMA((n // 2,)),
            pltpu.SemaphoreType.DMA((n // 2,)),
            pltpu.SemaphoreType.DMA((n // 2,)),
            pltpu.SemaphoreType.DMA,
            pltpu.SemaphoreType.DMA,
        ],
        compiler_params=pltpu.CompilerParams(
            collective_id=0, has_side_effects=True, vmem_limit_bytes=24 * 1024 * 1024
        ),
    )(counts, positives, seg_ids, ln_gain.reshape(1, width), tok, wout, ctx_t, w_proj)
    loss, grad = pl.pallas_call(
        functools.partial(loss_kernel, n, slots),
        name="contrast",
        out_shape=[
            jax.ShapeDtypeStruct((slots,), F32),
            jax.ShapeDtypeStruct((slots, width), F32),
        ],
        in_specs=[vmem, vmem],
        out_specs=[vmem, vmem],
        scratch_shapes=[
            pltpu.VMEM((total, width + EXT), F32),
            pltpu.VMEM((total, embed), F32),
            pltpu.VMEM((total, 128), F32),
            pltpu.VMEM((total, total), F32),
            pltpu.VMEM((total, total), F32),
        ],
        compiler_params=pltpu.CompilerParams(
            vmem_limit_bytes=(24 if total <= 128 else 56) * 1024 * 1024
        ),
    )(gath, wproj)
    return loss, grad


def solution(mesh):
    return jax.shard_map(
        functools.partial(body, mesh.shape["dp"]),
        mesh=mesh,
        in_specs=(P("dp", None), P("dp", None), P(), P("dp"), P(), P(), P(), P()),
        out_specs=(P("dp"), P("dp", None)),
        check_vma=False,
    )
```

time: 40.5 us -> 32.5 us (0.80)
  Pallas kernels: 38.9 us -> 31.7 us
  local copies, waits for them, and re-layouts: 0.7 us -> 0.02 us
    pallas_call x1, Pallas kernels: 23.6 us -> 13.8 us  [body(): pl.pallas_call(functools.partial(attend_kernel, block, slots), name='atte...]
    pallas_call x1, Pallas kernels: 11.6 us -> 14.2 us  [body(): pl.pallas_call(functools.partial(exchange_kernel, n, slots, block), name=...]
    unnamed x4 -> x8, local copies, waits for them, and re-layouts: 0.7 us -> 0.02 us
where the time goes in v1:
time: 32.5 us
  Pallas kernels  31.7 us (98%)
  between operations  0.71 us (2%)
    pallas_call x1, Pallas kernels, body(): pl.pallas_call(functools.partial(exchange_kernel, n, slots, block), name=...  14.2 us
    pallas_call x1, Pallas kernels, body(): pl.pallas_call(functools.partial(attend_kernel, block, slots), name='atte...  13.8 us
    pallas_call x1, Pallas kernels, body(): pl.pallas_call(functools.partial(loss_kernel, n, slots), name='contrast',...  3.76 us

profile of v1, /device:TPU:0, one launch (start us, length us, event | category | flops | bytes accessed | tf_op | source)
XLA Modules:
  0.0 32.5 jit_solution(12167276932813436615)
XLA Ops:
  0.6 0.0 copy-start
  0.6 0.0 copy-start.1
  0.7 0.0 copy-start.2
  0.7 0.0 copy-start.3
  0.7 13.8 %attend.1 = (bf16[1024,1024]{1,0:T(8,128)(2,1)S(1)}, bf16[512,1024]{1,0:T(8,128)(2,1)S(1)}, bf16[512,1024]{1,0:T(8,128)(2,1)S(1)}) custom-call(s32[1,1024]{1,0:T(1,128)} %seg_ref.1, bf16[1024,1024]{1,0:T(8,128)(2,1)} %tok_hbm.1, bf16[1024,1536]{1,0:T(8,128)(2,1)} %wqkv_hbm.1, bf16[512,1024]{1,0:T(8,128)(2,1)} %wout_hbm.1), custom_call_target="tpu_custom_call" | custom-call | tf_op jit(solution)/shard_map/attend/pallas_call | solution.py:330
  14.4 0.0 copy-done
  14.5 0.0 copy-done.1
  14.5 0.0 copy-done.2
  14.5 0.0 copy-done.3
  14.5 14.2 %exchange.1 = (bf16[32,4,1152]{2,1,0:T(4,128)(2,1)S(1)}, bf16[1024,2048]{1,0:T(8,128)(2,1)S(1)}) custom-call(s32[32]{0:T(128)S(1)} %copy-done.2, s32[4]{0:T(128)S(1)} %copy-done.3, s32[1,1024]{1,0:T(1,128)S(1)} %copy-done, f32[1,1024]{1,0:T(1,128)S(1)} %bitcast.1, bf16[1024,1024]{1,0:T(8,128)(2,1)S(1)} %get-tuple-element.7.tok, ...), custom_call_target="tpu_custom_call" | custom-call | tf_op jit(solution)/shard_map/exchange/pallas_call | solution.py:353
  28.7 3.8 %contrast.1 = (f32[4]{0:T(128)}, f32[4,1024]{1,0:T(4,128)}) custom-call(bf16[32,4,1152]{2,1,0:T(4,128)(2,1)S(1)} %get-tuple-element.10.gath, bf16[1024,2048]{1,0:T(8,128)(2,1)S(1)} %get-tuple-element.11.wproj), custom_call_target="tpu_custom_call" | custom-call | tf_op jit(solution)/shard_map/contrast/pallas_call | solution.py:376
Async XLA Ops:
  0.6 13.8 %copy-start = (s32[1,1024]{1,0:T(1,128)S(1)}, s32[1,1024]{1,0:T(1,128)}, u32[]{:S(2)}) copy-start(s32[1,1024]{1,0:T(1,128)} %seg_ref.1) | copy-start | bytes 12292
  0.6 13.8 %copy-start.1 = (f32[1024]{0:T(1024)S(1)}, f32[1024]{0:T(1024)}, u32[]{:S(2)}) copy-start(f32[1024]{0:T(1024)} %param.14) | copy-start | bytes 12292
  0.7 13.8 %copy-start.2 = (s32[32]{0:T(128)S(1)}, s32[32]{0:T(128)}, u32[]{:S(2)}) copy-start(s32[32]{0:T(128)} %counts_ref.1) | copy-start | bytes 388
  0.7 13.8 %copy-start.3 = (s32[4]{0:T(128)S(1)}, s32[4]{0:T(128)}, u32[]{:S(2)}) copy-start(s32[4]{0:T(128)} %pos_ref.1) | copy-start | bytes 52

commit v2 on v1

--- a/solution.py
+++ b/solution.py
@@ -14,7 +14,7 @@
 BF16 = jnp.bfloat16
 EXT = 128
 ONES_ROWS = 16
-GROUP = 1024
+FINISH = 1024
 LOG2E = 1.4426950408889634
 
 
@@ -26,7 +26,7 @@
     block, slots,
     seg_hbm, tok_hbm, wqkv_hbm, wout_hbm,
     tok, wout, ctx_t,
-    seg_ref, wqkv, qkv, vt, hot, far, s_buf, sem_tok, sem_w,
+    seg_ref, wqkv, qt, kd, vt, hot, far, s_buf, sem_tok, sem_w,
 ):
     rows, width = tok.shape
     inner = wout.shape[0]
@@ -49,53 +49,56 @@
     seg_copy = pltpu.make_async_copy(seg_hbm, seg_ref, sem_w.at[4])
     seg_copy.start()
     tok_copies[0].start()
-    w_copies[0].start()
-    for c in tok_copies[1:] + w_copies[1:]:
+    w_copies[1].start()
+    for c in tok_copies[1:] + [w_copies[0], w_copies[2]]:
         c.start()
     o_copy.start()
 
     seg_copy.wait()
     seg = seg_ref[...]
-    lane = lax.broadcasted_iota(jnp.int32, (rows, 128), 1)
-    seg_col = jnp.transpose(jnp.broadcast_to(seg.astype(F32), (128, rows))).astype(jnp.int32)
-    hot[...] = jnp.where(seg_col == lane, 1.0, 0.0).astype(BF16)
-    far[...] = jnp.where((lane < slots) & (seg_col != lane), -1e30, 0.0).astype(BF16)
+    slot = lax.broadcasted_iota(jnp.int32, (128, rows), 0)
+    hot[...] = jnp.transpose(jnp.where(slot == seg, 1.0, 0.0).astype(BF16))
+    far[...] = jnp.where((slot < slots) & (slot != seg), -1e30, 0.0).astype(BF16)
     starts = [
         jnp.sum(jnp.where(seg < s, 1.0, 0.0)).astype(jnp.int32) for s in range(1, slots)
     ]
 
-    for j in range(3):
+    for j in (1, 0, 2):
         w_copies[j].wait()
         cols = slice(j * inner, (j + 1) * inner)
-        for i in range(blocks):
-            if j == 0:
+        tall = block if j == 1 else min(2 * block, rows)
+        for i in range(rows // tall):
+            if j == 1:
                 tok_copies[i].wait()
-            r = slice(i * block, (i + 1) * block)
+            r = slice(i * tall, (i + 1) * tall)
             part = jnp.dot(tok[r, :], wqkv[:, cols], preferred_element_type=F32).astype(BF16)
             if j == 0:
-                qkv[r, cols] = (part.astype(F32) * head_dim ** (-0.5)).astype(BF16)
+                q = (part.astype(F32) * head_dim ** (-0.5)).astype(BF16)
+                qt[:, r] = jnp.transpose(q)
             elif j == 1:
-                qkv[r, cols] = part
+                kd[r, :] = part
             else:
                 vt[:, r] = jnp.transpose(part)
 
-    pair_lane = lax.broadcasted_iota(jnp.int32, (block, 128), 1)
-
     def attend(count, qr, base):
         bounds = [(c, min(c + block, count * 128)) for c in range(0, count * 128, block)]
 
         def query(h):
-            lo = (h * head_dim) // 128 * 128
-            own = (pair_lane >= h * head_dim - lo) & (pair_lane < (h + 1) * head_dim - lo)
-            q = jnp.where(own, qkv[qr, lo : lo + 128], jnp.zeros((), BF16))
-            return jnp.concatenate([q, far[qr, :]], axis=1)
+            hr = slice(h * head_dim, (h + 1) * head_dim)
+            lo = h * head_dim % 128
+            parts = [qt[hr, qr], far[:, qr]]
+            if lo:
+                parts.insert(0, jnp.zeros((lo, block), BF16))
+            if lo + head_dim < 128:
+                parts.insert(-1, jnp.zeros((128 - lo - head_dim, block), BF16))
+            return jnp.concatenate(parts, axis=0)
 
         def score(h, q_ext, c):
-            lo = inner + (h * head_dim) // 128 * 128
             a, b = bounds[c]
             kr = pl.ds(pl.multiple_of(base + a, 128), b - a)
-            k_ext = jnp.concatenate([qkv[kr, lo : lo + 128], hot[kr, :]], axis=1)
-            part = dot(k_ext, q_ext, 1, 1)
+            lo = h * head_dim // 128 * 128
+            k_ext = jnp.concatenate([kd[kr, lo : lo + 128], hot[kr, :]], axis=1)
+            part = jnp.dot(k_ext, q_ext, preferred_element_type=F32)
             s_buf[h % 2, a:b, :] = part
             return jnp.max(part, axis=0, keepdims=True)
 
@@ -145,7 +148,7 @@
 
 
 def exchange_kernel(
-    n, slots, block,
+    n, slots,
     counts_ref, pos_ref, seg_ref, gain_ref, tok, wout, ctx_t, wproj_hbm,
     gath, wproj,
     msg_ref, sums, send_sem, recv_sem, fwd_sem, got_sem, own_sem, w_sem,
@@ -170,7 +173,7 @@
     w_copy = pltpu.make_async_copy(wproj_hbm, wproj, w_sem)
     w_copy.start()
 
-    total_sum = None
+    block = min(FINISH, rows)
     for i in range(rows // block):
         qr = slice(i * block, (i + 1) * block)
         resid = tok[qr, :].astype(F32) + dot(ctx_t[:, qr], wout[...], 0, 0)
@@ -298,10 +301,9 @@
     wts_t[...] = jnp.transpose(weights)
 
     base = pl.ds(pl.multiple_of(me // per * 8, 8), 8)
-    d_emb = LOGIT_SCALE * (
-        jnp.dot(wts[base, :].astype(BF16), emb, preferred_element_type=F32)
-        + jnp.dot(wts_t[base, :].astype(BF16), emb, preferred_element_type=F32)
-    )
+    both = jnp.concatenate([wts[base, :], wts_t[base, :]], axis=0).astype(BF16)
+    parts = jnp.dot(both, emb, preferred_element_type=F32)
+    d_emb = LOGIT_SCALE * (parts[:8] + parts[8:])
     unit_own = unit[base, :]
     radial = jnp.sum(d_emb * unit_own, axis=-1, keepdims=True)
     d_proj = ((d_emb - radial * unit_own) * scale[base, :][:, :1]).astype(BF16)
@@ -340,10 +342,11 @@
         scratch_shapes=[
             pltpu.VMEM((1, rows), jnp.int32),
             pltpu.VMEM(w_qkv.shape, BF16),
-            pltpu.VMEM((rows, 2 * inner), BF16),
+            pltpu.VMEM((inner, rows), BF16),
+            pltpu.VMEM((rows, inner), BF16),
             pltpu.VMEM((inner, rows), BF16),
             pltpu.VMEM((rows, 128), BF16),
-            pltpu.VMEM((rows, 128), BF16),
+            pltpu.VMEM((128, rows), BF16),
             pltpu.VMEM((2, rows, block), F32),
             pltpu.SemaphoreType.DMA((rows // block,)),
             pltpu.SemaphoreType.DMA((5,)),
@@ -351,7 +354,7 @@
         compiler_params=pltpu.CompilerParams(vmem_limit_bytes=32 * 1024 * 1024),
     )(seg_hbm, tokens, w_qkv, w_out)
     gath, wproj = pl.pallas_call(
-        functools.partial(exchange_kernel, n, slots, block),
+        functools.partial(exchange_kernel, n, slots),
         name="exchange",
         out_shape=[
             jax.ShapeDtypeStruct((n, slots, width + EXT), BF16),

time: 32.5 us -> 31.4 us (0.966)
  Pallas kernels: 31.7 us -> 30.8 us
    pallas_call x1, Pallas kernels: 13.8 us -> 11.5 us  [body(): pl.pallas_call(functools.partial(attend_kernel, block, slots), name='atte...]
    pallas_call x1, Pallas kernels: 14.2 us -> 15.7 us  [body(): pl.pallas_call(functools.partial(exchange_kernel, n, slots), name='exchan...]
where the time goes in v2:
time: 31.4 us; the launch traced here: 31.6 us
  Pallas kernels  30.8 us (98%)
  between operations  0.71 us (2%)
    pallas_call x1, Pallas kernels, body(): pl.pallas_call(functools.partial(exchange_kernel, n, slots), name='exchan...  15.7 us
    pallas_call x1, Pallas kernels, body(): pl.pallas_call(functools.partial(attend_kernel, block, slots), name='atte...  11.5 us
    pallas_call x1, Pallas kernels, body(): pl.pallas_call(functools.partial(loss_kernel, n, slots), name='contrast',...  3.66 us

profile of v2, /device:TPU:0, one launch (start us, length us, event | category | flops | bytes accessed | tf_op | source)
XLA Modules:
  0.0 31.6 jit_solution(7441640922425513978)
XLA Ops:
  0.6 0.0 copy-start
  0.6 0.0 copy-start.1
  0.7 0.0 copy-start.2
  0.7 0.0 copy-start.3
  0.7 11.5 %attend.1 = (bf16[1024,1024]{1,0:T(8,128)(2,1)S(1)}, bf16[512,1024]{1,0:T(8,128)(2,1)S(1)}, bf16[512,1024]{1,0:T(8,128)(2,1)S(1)}) custom-call(s32[1,1024]{1,0:T(1,128)} %seg_ref.1, bf16[1024,1024]{1,0:T(8,128)(2,1)} %tok_hbm.1, bf16[1024,1536]{1,0:T(8,128)(2,1)} %wqkv_hbm.1, bf16[512,1024]{1,0:T(8,128)(2,1)} %wout_hbm.1), custom_call_target="tpu_custom_call" | custom-call | tf_op jit(solution)/shard_map/attend/pallas_call | solution.py:332
  12.1 0.0 copy-done
  12.2 0.0 copy-done.1
  12.2 0.0 copy-done.2
  12.2 0.0 copy-done.3
  12.2 15.7 %exchange.1 = (bf16[32,4,1152]{2,1,0:T(4,128)(2,1)S(1)}, bf16[1024,2048]{1,0:T(8,128)(2,1)S(1)}) custom-call(s32[32]{0:T(128)S(1)} %copy-done.2, s32[4]{0:T(128)S(1)} %copy-done.3, s32[1,1024]{1,0:T(1,128)S(1)} %copy-done, f32[1,1024]{1,0:T(1,128)S(1)} %bitcast.1, bf16[1024,1024]{1,0:T(8,128)(2,1)S(1)} %get-tuple-element.7.tok, ...), custom_call_target="tpu_custom_call" | custom-call | tf_op jit(solution)/shard_map/exchange/pallas_call | solution.py:356
  27.9 3.7 %contrast.1 = (f32[4]{0:T(128)}, f32[4,1024]{1,0:T(4,128)}) custom-call(bf16[32,4,1152]{2,1,0:T(4,128)(2,1)S(1)} %get-tuple-element.10.gath, bf16[1024,2048]{1,0:T(8,128)(2,1)S(1)} %get-tuple-element.11.wproj), custom_call_target="tpu_custom_call" | custom-call | tf_op jit(solution)/shard_map/contrast/pallas_call | solution.py:379
Async XLA Ops:
  0.6 11.5 %copy-start = (s32[1,1024]{1,0:T(1,128)S(1)}, s32[1,1024]{1,0:T(1,128)}, u32[]{:S(2)}) copy-start(s32[1,1024]{1,0:T(1,128)} %seg_ref.1) | copy-start | bytes 12292
  0.6 11.5 %copy-start.1 = (f32[1024]{0:T(1024)S(1)}, f32[1024]{0:T(1024)}, u32[]{:S(2)}) copy-start(f32[1024]{0:T(1024)} %param.14) | copy-start | bytes 12292
  0.7 11.5 %copy-start.2 = (s32[32]{0:T(128)S(1)}, s32[32]{0:T(128)}, u32[]{:S(2)}) copy-start(s32[32]{0:T(128)} %counts_ref.1) | copy-start | bytes 388
  0.7 11.5 %copy-start.3 = (s32[4]{0:T(128)S(1)}, s32[4]{0:T(128)}, u32[]{:S(2)}) copy-start(s32[4]{0:T(128)} %pos_ref.1) | copy-start | bytes 52

commit v3 on v2

--- a/solution.py
+++ b/solution.py
@@ -134,17 +134,34 @@
         first = lo // 128
         count = (hi + 127) // 128 - first
         qr = pl.ds(pl.multiple_of(begin, block), block)
-        base = first * 128
-        for n in range(block // 128, rows // 128 + 1):
-
-            @pl.when(count == n)
+        most = rows // 128
+        sizes = sorted({min(n, most) for n in (2, 3, 4, 5, 6)} | {most})
+        below = 0
+        for n in sizes:
+
+            @pl.when((count > below) & (count <= n))
             def _():
-                attend(n, qr, base)
+                attend(n, qr, jnp.minimum(first, most - n) * 128)
+
+            below = n
 
         return carry
 
     lax.fori_loop(0, blocks, step, 0)
     o_copy.wait()
+
+
+def each(first, last, f):
+    if last - first <= 16:
+        for m in range(first, last):
+            f(m)
+        return
+
+    def one(m, c):
+        f(m)
+        return c
+
+    lax.fori_loop(first, last, one, 0)
 
 
 def exchange_kernel(
@@ -162,13 +179,13 @@
     barrier = pltpu.get_barrier_semaphore()
 
     def peer_of(d):
-        return lax.rem(chip + d, chips) * 2 + core
-
-    def greet(d, c):
+        ahead = chip + d
+        return jnp.where(ahead < chips, ahead, ahead - chips) * 2 + core
+
+    def greet(d):
         pl.semaphore_signal(barrier, inc=1, device_id=(peer_of(d),), device_id_type=MESH)
-        return c
-
-    lax.fori_loop(1, chips, greet, 0)
+
+    each(1, chips, greet)
     pl.semaphore_signal(barrier, inc=1, device_id=(other,), device_id_type=MESH)
     w_copy = pltpu.make_async_copy(wproj_hbm, wproj, w_sem)
     w_copy.start()
@@ -214,7 +231,8 @@
         )
 
     def relay(d):
-        src = lax.rem(chip + chips - d, chips) * 2 + core
+        back = chip - d
+        src = jnp.where(back < 0, back + chips, back) * 2 + core
         return pltpu.make_async_remote_copy(
             src_ref=gath.at[src], dst_ref=gath.at[src],
             send_sem=fwd_sem.at[d], recv_sem=got_sem.at[d],
@@ -227,26 +245,20 @@
         device_id=(other,), device_id_type=MESH,
     )
 
-    def send(d, c):
-        send_to(d).start()
-        return c
-
-    def forward(d, c):
+    def forward(d):
         send_to(d).wait_recv()
         relay(d).start()
-        return c
-
-    def arrive(d, c):
+
+    def arrive(d):
         send_to(d).wait_send()
         relay(d).wait()
-        return c
-
-    lax.fori_loop(1, chips, send, 0)
+
+    each(1, chips, lambda d: send_to(d).start())
     mine.start()
-    lax.fori_loop(1, chips, forward, 0)
+    each(1, chips, forward)
     own.wait()
     mine.wait()
-    lax.fori_loop(1, chips, arrive, 0)
+    each(1, chips, arrive)
     w_copy.wait()
 
 
@@ -261,12 +273,11 @@
     width = wproj.shape[0]
     per = 8 // slots
 
-    def place(i, c):
+    def place(i):
         group = [gath[i * per + k].astype(F32) for k in range(per)]
         allp[pl.ds(pl.multiple_of(i * 8, 8), 8), :] = jnp.concatenate(group, axis=0)
-        return c
-
-    lax.fori_loop(0, total // 8, place, 0)
+
+    each(0, total // 8, place)
 
     pooled = allp[:, :width].astype(BF16)
     ext = allp[:, width:]

time: 31.4 us -> 30.8 us (0.981); the launches traced: 31.6 us -> 30.6 us
  Pallas kernels: 30.8 us -> 29.8 us
    pallas_call x1, Pallas kernels: 15.7 us -> 14.9 us  [body(): pl.pallas_call(functools.partial(exchange_kernel, n, slots), name='exchan...]
where the time goes in v3:
time: 30.8 us; the launch traced here: 30.6 us
  Pallas kernels  29.8 us (97%)
  between operations  0.71 us (2%)
    pallas_call x1, Pallas kernels, body(): pl.pallas_call(functools.partial(exchange_kernel, n, slots), name='exchan...  14.9 us
    pallas_call x1, Pallas kernels, body(): pl.pallas_call(functools.partial(attend_kernel, block, slots), name='atte...  11.5 us
    pallas_call x1, Pallas kernels, body(): pl.pallas_call(functools.partial(loss_kernel, n, slots), name='contrast',...  3.53 us

profile of v3, /device:TPU:0, one launch (start us, length us, event | category | flops | bytes accessed | tf_op | source)
XLA Modules:
  0.0 30.6 jit_solution(12660422005970457320)
XLA Ops:
  0.6 0.0 copy-start
  0.6 0.0 copy-start.1
  0.7 0.0 copy-start.2
  0.7 0.0 copy-start.3
  0.7 11.5 %attend.1 = (bf16[1024,1024]{1,0:T(8,128)(2,1)S(1)}, bf16[512,1024]{1,0:T(8,128)(2,1)S(1)}, bf16[512,1024]{1,0:T(8,128)(2,1)S(1)}) custom-call(s32[1,1024]{1,0:T(1,128)} %seg_ref.1, bf16[1024,1024]{1,0:T(8,128)(2,1)} %tok_hbm.1, bf16[1024,1536]{1,0:T(8,128)(2,1)} %wqkv_hbm.1, bf16[512,1024]{1,0:T(8,128)(2,1)} %wout_hbm.1), custom_call_target="tpu_custom_call" | custom-call | tf_op jit(solution)/shard_map/attend/pallas_call | solution.py:343
  12.1 0.0 copy-done
  12.1 0.0 copy-done.1
  12.2 0.0 copy-done.2
  12.2 0.0 copy-done.3
  12.2 14.9 %exchange.1 = (bf16[32,4,1152]{2,1,0:T(4,128)(2,1)S(1)}, bf16[1024,2048]{1,0:T(8,128)(2,1)S(1)}) custom-call(s32[32]{0:T(128)S(1)} %copy-done.2, s32[4]{0:T(128)S(1)} %copy-done.3, s32[1,1024]{1,0:T(1,128)S(1)} %copy-done, f32[1,1024]{1,0:T(1,128)S(1)} %bitcast.1, bf16[1024,1024]{1,0:T(8,128)(2,1)S(1)} %get-tuple-element.7.tok, ...), custom_call_target="tpu_custom_call" | custom-call | tf_op jit(solution)/shard_map/exchange/pallas_call | solution.py:367
  27.0 3.5 %contrast.1 = (f32[4]{0:T(128)}, f32[4,1024]{1,0:T(4,128)}) custom-call(bf16[32,4,1152]{2,1,0:T(4,128)(2,1)S(1)} %get-tuple-element.10.gath, bf16[1024,2048]{1,0:T(8,128)(2,1)S(1)} %get-tuple-element.11.wproj), custom_call_target="tpu_custom_call" | custom-call | tf_op jit(solution)/shard_map/contrast/pallas_call | solution.py:390
Async XLA Ops:
  0.6 11.5 %copy-start = (s32[1,1024]{1,0:T(1,128)S(1)}, s32[1,1024]{1,0:T(1,128)}, u32[]{:S(2)}) copy-start(s32[1,1024]{1,0:T(1,128)} %seg_ref.1) | copy-start | bytes 12292
  0.6 11.5 %copy-start.1 = (f32[1024]{0:T(1024)S(1)}, f32[1024]{0:T(1024)}, u32[]{:S(2)}) copy-start(f32[1024]{0:T(1024)} %param.14) | copy-start | bytes 12292
  0.7 11.5 %copy-start.2 = (s32[32]{0:T(128)S(1)}, s32[32]{0:T(128)}, u32[]{:S(2)}) copy-start(s32[32]{0:T(128)} %counts_ref.1) | copy-start | bytes 388
  0.7 11.5 %copy-start.3 = (s32[4]{0:T(128)S(1)}, s32[4]{0:T(128)}, u32[]{:S(2)}) copy-start(s32[4]{0:T(128)} %pos_ref.1) | copy-start | bytes 52
